TPU v7x, 32 devices: a whole 2x2x4 slice. The times are simulated.
32 devices in a mesh: heads: 2 (over x), seq: 16 (over z, y, core).
Axes of the slice: x: 2, y: 2, z: 4, core: 2. Of those that a mesh axis runs over, the one named last changes fastest.
Arguments:
- query_nope: bfloat16 [1, 4, 128, 128], P(None, None, 'heads'), may hold values from -6 to 6
- query_rope: bfloat16 [1, 4, 128, 64], P(None, None, 'heads'), may hold values from -8 to 8
- latent_cache: bfloat16 [1, 8192, 512], P(None, 'seq'), may hold values from -6 to 6
- rope_keys: bfloat16 [1, 64, 8192], P(None, None, 'seq'), may hold values from -8 to 8
- lengths: int32 [1], replicated, may hold values from 2 to 8189, as said below
- key_quant: bfloat16 [128, 512, 128], P('heads', 'seq'), may hold values from -127 to 127, as said below
- key_scale: float32 [128, 4], P('heads'), may hold values from 0.0006 to 0.0024
- value_quant: bfloat16 [128, 512, 128], P('heads', 'seq'), may hold values from -127 to 127, as said below
- value_scale: float32 [128, 4], P('heads'), may hold values from 0.0003 to 0.0012
- out_weight: bfloat16 [16384, 7168], P('heads', 'seq'), may hold values from -0.375 to 0.375
Outputs:
- attn_out: bfloat16 [1, 4, 7168], P(None, None, 'seq')
Inputs may be any that keep to these rules, and one draw needn't show every extreme that they name: `key_quant`: whole numbers. `value_quant`: whole numbers. `lengths`: one sequence has the largest allowed length, so that its last draft token sees all 8192 positions.
All inputs are finite; a program needn't handle non-finite values.
Results may differ from a plain program's by a relative error of at most 0.019.
Values may be sent and summed in bfloat16 or wider, within the bound.
A program may use at most 64 MiB of HBM per device.

v0:
```python
import jax
import jax.numpy as jnp
from jax import lax
from jax.sharding import PartitionSpec as P

QB = 128


neg_large = -1e30


def expand_scales(block_scale, offset, count):
    row_ids = (offset + jnp.arange(count, dtype=jnp.int32)) // QB
    onehot = (
        row_ids[:, None] == jnp.arange(block_scale.shape[1], dtype=jnp.int32)[None, :]
    ).astype(block_scale.dtype)
    return jnp.sum(block_scale[:, None, :] * onehot[None, :, :], axis=2)


def dequantize(quantized, block_scale, offset):
    factors = expand_scales(block_scale, offset, quantized.shape[1])
    return (quantized.astype(jnp.float32) * factors[:, :, None]).astype(jnp.bfloat16)


def per_device(
    query_nope,
    query_rope,
    latent_cache,
    rope_keys,
    lengths,
    key_quant,
    key_scale,
    value_quant,
    value_scale,
    out_weight,
):
    seq_index = lax.axis_index("seq")
    latent_cols = key_quant.shape[1]
    offset = seq_index * latent_cols
    factor = (query_nope.shape[-1] + query_rope.shape[-1]) ** (-0.5)
    key_weight = dequantize(key_quant, key_scale, offset)
    piece_lat = jnp.einsum(
        "btkn,kcn->btkc", query_nope, key_weight, preferred_element_type=jnp.float32
    ).astype(jnp.bfloat16)
    query_latent = lax.all_gather(piece_lat, "seq", axis=3, tiled=True)
    positions = latent_cache.shape[1]
    scores = jnp.einsum(
        "btkc,bsc->btks", query_latent, latent_cache, preferred_element_type=jnp.float32
    )
    scores = (
        scores
        + jnp.einsum("btkr,brs->btks", query_rope, rope_keys, preferred_element_type=jnp.float32)
    ) * factor
    position = seq_index * positions + jnp.arange(positions, dtype=jnp.int32)
    horizon = lengths[:, None] + jnp.arange(query_nope.shape[1], dtype=jnp.int32)[None, :]
    visible = (position[None, None, :] < horizon[:, :, None])[:, :, None, :]
    block_max = jnp.max(jnp.where(visible, scores, neg_large), axis=3)
    probs = jnp.where(visible, jnp.exp(scores - block_max[..., None]), 0.0)
    block_sum = jnp.sum(probs, axis=3)
    probs_bf = probs.astype(jnp.bfloat16)
    block_out = jnp.einsum(
        "btks,bsc->btkc", probs_bf, latent_cache, preferred_element_type=jnp.float32
    )
    top = lax.pmax(block_max, "seq")
    rescale = jnp.exp(block_max - top)
    totals = lax.psum(block_sum * rescale, "seq")
    shrink = jnp.exp(block_max - top)
    merged_slice = lax.psum_scatter(
        block_out * shrink[..., None], "seq", scatter_dimension=3, tiled=True
    )
    latent_slice = (merged_slice / totals[..., None]).astype(jnp.bfloat16)
    value_weight = dequantize(value_quant, value_scale, offset)
    partial_heads = jnp.einsum(
        "btkc,kcv->btkv", latent_slice, value_weight, preferred_element_type=jnp.float32
    )
    flat_terms = partial_heads.reshape(-1)
    share_sum = lax.psum_scatter(flat_terms, "seq", scatter_dimension=0, tiled=True).astype(
        jnp.bfloat16
    )
    head_output = lax.all_gather(share_sum, "seq", axis=0, tiled=True).reshape(partial_heads.shape)
    batch, drafts, heads_here, value_width = head_output.shape
    projected = jnp.dot(
        head_output.reshape(batch * drafts, heads_here * value_width),
        out_weight,
        preferred_element_type=jnp.float32,
    )
    summed = lax.psum(projected, "heads")
    return summed.astype(jnp.bfloat16).reshape(batch, drafts, out_weight.shape[1])


def solution(mesh):
    in_specs = (
        P(None, None, "heads", None),
        P(None, None, "heads", None),
        P(None, "seq", None),
        P(None, None, "seq"),
        P(),
        P("heads", "seq", None),
        P("heads", None),
        P("heads", "seq", None),
        P("heads", None),
        P("heads", "seq"),
    )
    out_specs = P(None, None, "seq")
    return jax.shard_map(
        per_device, mesh=mesh, in_specs=in_specs, out_specs=out_specs, check_vma=False
    )
```

profile of v0, /device:TPU:0, one launch (start us, length us, event | category | flops | bytes accessed | tf_op | source)
XLA Modules:
  0.0 255.0 jit_solution(11461911653005468374)
XLA Ops:
  6.5 0.0 copy-start
  6.5 0.0 copy-start.2
  6.5 0.0 copy-start.1
  6.5 0.0 all-reduce.5.cloned.1.call-start
  7.3 0.8 multiply_reduce_fusion.1
  8.1 0.1 copy.31
  8.2 1.5 fusion.2
  9.7 0.1 copy.33
  9.8 24.6 %all_gather.6 = bf16[1,4,64,512]{2,1,0,3:T(4,128)(2,1)S(1)} all-gather(bf16[1,4,64,32]{2,1,0,3:T(4,128)(2,1)S(1)} %copy.33), channel_id=1, replica_groups=mesh['heads'=2,'seq'=16] {'seq'}, dimensions={3}, use_global_device_ids=true | all-gather | bytes 278528 | tf_op jit(solution)/shard_map/all_gather | solution.py:45
  34.4 0.3 copy.34
  34.7 0.1 broadcast_compare_fusion
  34.8 0.0 copy-done
  34.8 0.3 fusion.4
  35.2 1.2 select_reduce_fusion
  36.3 29.8 %pmax.7 = f32[1,4,64]{2,1,0:T(4,128)S(1)} all-reduce(f32[1,4,64]{2,1,0:T(4,128)S(1)} %bitcast.55), channel_id=1, replica_groups=mesh['heads'=2,'seq'=16] {'seq'}, use_global_device_ids=true, to_apply=%region_3.4 | all-reduce | flops 256 | bytes 2048 | tf_op jit(solution)/shard_map/pmax | solution.py:64
  66.2 0.2 fusion.8
  66.4 0.4 fusion.1
  66.8 1.4 copy.35
  68.1 0.0 all-reduce.5.cloned.1.call-update
  68.2 0.0 copy-done.2
  68.2 0.6 dynamic-slice
  69.4 0.1 copy.30
  70.2 29.5 %psum.14 = f32[4,64]{1,0:T(4,128)S(1)} all-reduce(f32[4,64]{1,0:T(4,128)S(1)} %get-tuple-element.8), channel_id=1, replica_groups=mesh['heads'=2,'seq'=16] {'seq'}, use_global_device_ids=true, to_apply=%region_6.7 | all-reduce | flops 256 | bytes 2048 | tf_op jit(solution)/shard_map/psum | solution.py:66
  99.7 59.7 %all-reduce.5.cloned.1.call-done = f32[1,4,64,512]{2,1,0,3:T(4,128)} async-done(((f32[1,4,64,512]{2,1,0,3:T(4,128)}), f32[1,4,64,512]{2,1,0,3:T(4,128)}) %all-reduce.5.cloned.1.call-update) | async-done | bytes 524304
  159.4 0.9 fusion.19
  160.2 0.1 copy.36
  160.4 0.0 copy-done.1
  160.4 0.4 convolution_bitcast_fusion
  160.8 59.3 %all-reduce.6 = bf16[32768]{0:T(1024)(128)(2,1)S(1)} all-reduce(f32[32768]{0:T(1024)S(1)} %bitcast.54), channel_id=3, replica_groups=mesh['heads'=2,'seq'=16] {'seq'}, use_global_device_ids=true, to_apply=%region_7.8.clone | all-reduce | flops 32768 | bytes 196608
  220.1 17.3 %all_gather.7 = bf16[32768]{0:T(1024)(128)(2,1)S(1)} all-gather(bf16[2048]{0:T(1024)(128)(2,1)S(1)} %dynamic-slice.10), channel_id=1, replica_groups=mesh['heads'=2,'seq'=16] {'seq'}, dimensions={0}, use_global_device_ids=true | all-gather | bytes 69632 | tf_op jit(solution)/shard_map/all_gather | solution.py:80
  237.5 5.1 %fusion.24 = f32[4,448]{1,0:T(4,128)S(1)} fusion(bf16[4,8192]{1,0:T(4,128)(2,1)S(1)} %reshape_reshape.3, bf16[8192,448]{0,1:T(8,128)(2,1)} %param.19), kind=kOutput, calls=%fused_computation.46 | convolution fusion | flops 29360128 | bytes 7412736 | tf_op jit(solution)/shard_map/dot_general | solution.py:82
  242.5 5.6 %psum.15 = bf16[4,448]{1,0:T(4,128)(2,1)} all-reduce(f32[4,448]{1,0:T(4,128)S(1)} %fusion.24), channel_id=1, replica_groups=mesh['heads'=2,'seq'=16] {'heads'}, use_global_device_ids=true, to_apply=%region_8.9 | all-reduce | flops 1792 | bytes 10752 | tf_op jit(solution)/shard_map/psum | solution.py:87
  (8 shorter events, 0.1 us)
Async XLA Ops:
  6.5 28.3 %copy-start = (bf16[1,512,512]{2,1,0:T(8,128)(2,1)S(1)}, bf16[1,512,512]{2,1,0:T(8,128)(2,1)}, u32[]{:S(2)}) copy-start(bf16[1,512,512]{2,1,0:T(8,128)(2,1)} %param.12) | copy-start | bytes 1572868
  6.5 61.6 %copy-start.2 = (u32[32]{0:T(128)S(1)}, u32[32]{0:T(128)}, u32[]{:S(2)}) copy-start(u32[32]{0:T(128)} %constant.36) | copy-start | bytes 388
  6.5 153.8 %copy-start.1 = (bf16[64,32,128]{2,1,0:T(8,128)(2,1)S(1)}, bf16[64,32,128]{2,1,0:T(8,128)(2,1)}, u32[]{:S(2)}) copy-start(bf16[64,32,128]{2,1,0:T(8,128)(2,1)} %param.17) | copy-start | bytes 1572868
  6.5 152.8 %all-reduce.5.cloned.1.call-start = ((), (), s32[]{:S(2)}) async-start(), calls=%async_computation | async-start | bytes 2097152
Sparse Core Ops, SparseCore 0:
  68.3 91.0 all-reduce.4
where the time goes:
time: 255 us
  blocking collectives  166 us (65%)
  waiting for transfers between devices  59.7 us (23%)
  between operations  15.6 us (6%)
  matrix products  8.86 us (3%)
  local copies, waits for them, and re-layouts  2.7 us (1%)
    unnamed x2, waiting for transfers between devices  59.7 us
    unnamed x1, blocking collectives  59.3 us
    pmax x1, blocking collectives, per_device(): top = lax.pmax(block_max, 'seq')  29.8 us
    psum x1, blocking collectives, per_device(): totals = lax.psum(block_sum * rescale, 'seq')  29.5 us
    all_gather x1, blocking collectives, per_device(): query_latent = lax.all_gather(piece_lat, 'seq', axis=3, tiled=True)  24.6 us
    all_gather x1, blocking collectives, per_device(): lax.all_gather(share_sum, 'seq', axis=0, tiled=True)  17.3 us
    psum x1, blocking collectives, per_device(): summed = lax.psum(projected, 'heads')  5.57 us
  transfers between devices with their start and end apart: 1, of which 1 were waited for; matrix products, arithmetic and copies ran while one was open for 0% of the time, Pallas kernels for 0%

commit v1 on v0

v1 whole, which is shorter than its diff:
```python
import functools

import jax
import jax.numpy as jnp
from jax import lax
from jax.experimental import pallas as pl
from jax.experimental.pallas import tpu as pltpu
from jax.sharding import PartitionSpec as P

QB = 128
MESH = pl.DeviceIdType.MESH
neg_large = -1e30
F32 = jnp.float32
BF16 = jnp.bfloat16


def scale_row(scale_ref, block, rows, heads):
    scales = scale_ref[...]
    column = jnp.sum(
        jnp.where(lax.broadcasted_iota(jnp.int32, scales.shape, 1) == block, scales, 0.0),
        axis=1,
        keepdims=True,
    )
    lane_head = lax.broadcasted_iota(jnp.int32, (heads, rows), 1) % heads
    own_head = lax.broadcasted_iota(jnp.int32, (heads, rows), 0)
    return jnp.sum(jnp.where(lane_head == own_head, column, 0.0), axis=0, keepdims=True)


def kernel(
    n,
    groups,
    heads,
    drafts,
    q_hbm,
    qr_hbm,
    cache_hbm,
    rope_hbm,
    len_ref,
    kq_hbm,
    ks_ref,
    vq_hbm,
    vs_ref,
    w_hbm,
    out_ref,
    q,
    qr,
    cache,
    rope,
    kq,
    vq,
    w,
    cache_t,
    vq_t,
    base,
    lat_all,
    stats,
    out_send,
    out_recv,
    part_send,
    part_recv,
    share_all,
    flat,
    heads_out,
    final,
    in_sem,
    lat_send,
    lat_recv,
    st_send,
    st_recv,
    o_send,
    o_recv,
    p_send,
    p_recv,
    s_send,
    s_recv,
    f_send,
    f_recv,
):
    me = lax.axis_index("seq")
    group = lax.axis_index("heads")
    rows = q.shape[0]
    cols = lat_all.shape[1]
    width = vq.shape[1]
    positions = cache.shape[0]
    factor = (q.shape[1] + qr.shape[1]) ** (-0.5)

    loads = []
    for i, (src, dst) in enumerate(
        ((kq_hbm, kq), (q_hbm, q), (qr_hbm, qr), (rope_hbm, rope), (cache_hbm, cache), (vq_hbm, vq), (w_hbm, w))
    ):
        copy = pltpu.make_async_copy(src, dst, in_sem.at[i])
        copy.start()
        loads.append(copy)
    kq_load, q_load, qr_load, rope_load, cache_load, vq_load, w_load = loads

    barrier = pltpu.get_barrier_semaphore()

    def greet_seq(j, c):
        pl.semaphore_signal(barrier, inc=1, device_id=(group, lax.rem(me + j, n)), device_id_type=MESH)
        return c

    def greet_heads(j, c):
        pl.semaphore_signal(barrier, inc=1, device_id=(lax.rem(group + j, groups), me), device_id_type=MESH)
        return c

    lax.fori_loop(1, n, greet_seq, 0)
    lax.fori_loop(1, groups, greet_heads, 0)

    def spread(src_of, dst, send, recv):
        def make(j):
            peer = lax.rem(me + j, n)
            return pltpu.make_async_remote_copy(
                src_ref=src_of(peer),
                dst_ref=dst.at[me],
                send_sem=send.at[peer],
                recv_sem=recv.at[me],
                device_id=(group, peer),
                device_id_type=MESH,
            )

        def go(j, c):
            make(j).start()
            return c

        lax.fori_loop(1, n, go, 0)

    def arrive(src_of, dst, send, recv):
        def wait(j, c):
            peer = lax.rem(me + j, n)
            pltpu.make_async_remote_copy(
                src_ref=src_of(peer),
                dst_ref=dst.at[peer],
                send_sem=send.at[peer],
                recv_sem=recv.at[peer],
                device_id=(group, peer),
                device_id_type=MESH,
            ).wait_recv()
            return c

        lax.fori_loop(1, n, wait, 0)

    def drain(src_of, dst, send, recv):
        def wait(j, c):
            peer = lax.rem(me + j, n)
            pltpu.make_async_remote_copy(
                src_ref=src_of(peer),
                dst_ref=dst.at[me],
                send_sem=send.at[peer],
                recv_sem=recv.at[me],
                device_id=(group, peer),
                device_id_type=MESH,
            ).wait_send()
            return c

        lax.fori_loop(1, n, wait, 0)

    block = (me * cols) // QB
    lane_head = lax.broadcasted_iota(jnp.int32, (1, rows), 1) % heads
    key_row = scale_row(ks_ref, block, rows, heads)
    value_row = scale_row(vs_ref, block, rows, heads)

    kq_load.wait()
    q_load.wait()
    every = lax.dot_general(kq[...], q[...], (((1,), (1,)), ((), ())), preferred_element_type=F32)
    every = every.reshape(heads, cols, rows)
    own = lax.broadcasted_iota(jnp.int32, (heads, 1, rows), 0) == lane_head[None]
    piece = jnp.sum(jnp.where(own, every, 0.0), axis=0) * key_row
    lat_all[me] = piece.astype(BF16)

    pl.semaphore_wait(barrier, n - 1 + groups - 1)
    lat = (lambda peer: lat_all.at[me], lat_all, lat_send, lat_recv)
    spread(*lat)

    qr_load.wait()
    rope_load.wait()
    base[...] = lax.dot_general(
        rope[...].T, qr[...], (((1,), (1,)), ((), ())), preferred_element_type=F32
    )
    cache_load.wait()
    cache_t[...] = cache[...].T
    vq_load.wait()
    vq_t[...] = vq[...].T
    position = me * positions + lax.broadcasted_iota(jnp.int32, (positions, rows), 0)
    horizon = len_ref[0] + lax.broadcasted_iota(jnp.int32, (positions, rows), 1) // heads
    visible = position < horizon

    arrive(*lat)
    query_latent = lat_all[...].reshape(n * cols, rows)
    scores = (jnp.dot(cache[...], query_latent, preferred_element_type=F32) + base[...]) * factor
    block_max = jnp.max(jnp.where(visible, scores, neg_large), axis=0, keepdims=True)
    probs = jnp.where(visible, jnp.exp(scores - block_max), 0.0)
    block_sum = jnp.sum(probs, axis=0, keepdims=True)
    stats[me, 0:1, :] = block_max
    stats[me, 1:2, :] = block_sum
    st = (lambda peer: stats.at[me], stats, st_send, st_recv)
    spread(*st)
    block_out = jnp.dot(cache_t[...], probs.astype(BF16), preferred_element_type=F32)
    out_send[...] = block_out.astype(BF16).reshape(n, cols, rows)
    o = (lambda peer: out_send.at[peer], out_recv, o_send, o_recv)
    spread(*o)
    out_recv[me] = out_send[me]

    arrive(*st)
    all_max = stats[:, 0:1, :]
    top = jnp.max(all_max, axis=0, keepdims=True)
    weight = jnp.exp(all_max - top)
    total = jnp.sum(weight * stats[:, 1:2, :], axis=0)
    arrive(*o)
    merged = jnp.sum(out_recv[...].astype(F32) * weight, axis=0) / total
    latent = jnp.where(own, merged[None], 0.0).astype(BF16).reshape(heads * cols, rows)
    partial = jnp.dot(vq_t[...], latent, preferred_element_type=F32) * value_row
    step = width // n
    for d in range(n):
        part_send[d] = partial[d * step : (d + 1) * step].astype(part_send.dtype)
    p = (lambda peer: part_send.at[peer], part_recv, p_send, p_recv)
    spread(*p)
    part_recv[me] = part_send[me]
    arrive(*p)
    share_all[me] = jnp.sum(part_recv[...].astype(F32), axis=0).astype(BF16)
    s = (lambda peer: share_all.at[me], share_all, s_send, s_recv)
    spread(*s)
    arrive(*s)
    head_t = jnp.concatenate([share_all[d].astype(F32) for d in range(n)], axis=0)
    heads_out[...] = head_t.T.reshape(drafts, heads, width)
    for k in range(heads):
        flat[:, k * width : (k + 1) * width] = heads_out[:, k, :].astype(BF16)
    w_load.wait()
    final[group] = jnp.dot(flat[...], w[...], preferred_element_type=F32)

    def pair(j, at):
        peer = lax.rem(group + j, groups)
        return pltpu.make_async_remote_copy(
            src_ref=final.at[group],
            dst_ref=final.at[group if at else peer],
            send_sem=f_send.at[peer],
            recv_sem=f_recv.at[group if at else peer],
            device_id=(peer, me),
            device_id_type=MESH,
        )

    for j in range(1, groups):
        pair(j, True).start()
    for j in range(1, groups):
        pair(j, False).wait_recv()
    out_ref[...] = jnp.sum(final[...], axis=0).astype(BF16)
    for each in (lat, st, o, p, s):
        drain(*each)
    for j in range(1, groups):
        pair(j, True).wait_send()


def solution(mesh):
    n = mesh.shape["seq"]
    groups = mesh.shape["heads"]

    def per_device(
        query_nope,
        query_rope,
        latent_cache,
        rope_keys,
        lengths,
        key_quant,
        key_scale,
        value_quant,
        value_scale,
        out_weight,
    ):
        batch, drafts, heads, nope = query_nope.shape
        rows = batch * drafts * heads
        rope = query_rope.shape[-1]
        positions, latent = latent_cache.shape[1:]
        cols = key_quant.shape[1]
        width = value_quant.shape[2]
        model = out_weight.shape[1]
        hbm = pl.BlockSpec(memory_space=pltpu.HBM)
        vmem = pl.BlockSpec(memory_space=pltpu.VMEM)
        smem = pl.BlockSpec(memory_space=pltpu.SMEM)
        dma = pltpu.SemaphoreType.DMA
        result = pl.pallas_call(
            functools.partial(kernel, n, groups, heads, drafts),
            out_shape=jax.ShapeDtypeStruct((drafts, model), BF16),
            in_specs=[hbm, hbm, hbm, hbm, smem, hbm, vmem, hbm, vmem, hbm],
            out_specs=vmem,
            scratch_shapes=[
                pltpu.VMEM((rows, nope), BF16),
                pltpu.VMEM((rows, rope), BF16),
                pltpu.VMEM((positions, latent), BF16),
                pltpu.VMEM((rope, positions), BF16),
                pltpu.VMEM((heads * cols, nope), BF16),
                pltpu.VMEM((heads * cols, width), BF16),
                pltpu.VMEM(out_weight.shape, BF16),
                pltpu.VMEM((latent, positions), BF16),
                pltpu.VMEM((width, heads * cols), BF16),
                pltpu.VMEM((positions, rows), F32),
                pltpu.VMEM((n, cols, rows), BF16),
                pltpu.VMEM((n, 2, rows), F32),
                pltpu.VMEM((n, cols, rows), BF16),
                pltpu.VMEM((n, cols, rows), BF16),
                pltpu.VMEM((n, width // n, rows), BF16),
                pltpu.VMEM((n, width // n, rows), BF16),
                pltpu.VMEM((n, width // n, rows), BF16),
                pltpu.VMEM((drafts, heads * width), BF16),
                pltpu.VMEM((drafts, heads, width), F32),
                pltpu.VMEM((groups, drafts, model), F32),
                dma((7,)),
            ]
            + [dma((n,))] * 10
            + [dma((groups,))] * 2,
            compiler_params=pltpu.CompilerParams(
                collective_id=0, has_side_effects=True, vmem_limit_bytes=48 * 1024 * 1024
            ),
        )(
            query_nope.reshape(rows, nope),
            query_rope.reshape(rows, rope),
            latent_cache.reshape(positions, latent),
            rope_keys.reshape(rope, positions),
            lengths,
            key_quant.reshape(heads * cols, nope),
            key_scale,
            value_quant.reshape(heads * cols, width),
            value_scale,
            out_weight,
        )
        return result.reshape(batch, drafts, model)

    in_specs = (
        P(None, None, "heads", None),
        P(None, None, "heads", None),
        P(None, "seq", None),
        P(None, None, "seq"),
        P(),
        P("heads", "seq", None),
        P("heads", None),
        P("heads", "seq", None),
        P("heads", None),
        P("heads", "seq"),
    )
    return jax.shard_map(
        per_device, mesh=mesh, in_specs=in_specs, out_specs=P(None, None, "seq"), check_vma=False
    )
```

time: 255 us -> 52 us (0.20)
  blocking collectives: 166 us -> 0 us
  waiting for transfers between devices: 59.7 us -> 0 us
  Pallas kernels: 0 us -> 37.3 us
  between operations: 15.6 us -> 0.83 us
  local copies, waits for them, and re-layouts: 2.7 us -> 13.5 us
  matrix products: 8.86 us -> 0 us
    unnamed x2 -> x0, waiting for transfers between devices: 59.7 us -> none
    unnamed x1 -> x0, blocking collectives: 59.3 us -> none
    all_gather x2 -> x0, blocking collectives: 41.9 us -> none  [the longest x1 24.6 us: per_device(): query_latent = lax.all_gather(piece_lat, 'seq', axis=3, tiled=True)]
    pallas_call x0 -> x1, Pallas kernels: none -> 37.3 us  [per_device(): pl.pallas_call(functools.partial(kernel, n, groups, heads, drafts), out_s...]
    psum x2 -> x0, blocking collectives: 35.1 us -> none  [the longest x1 29.5 us: per_device(): totals = lax.psum(block_sum * rescale, 'seq')]
    pmax x1 -> x0, blocking collectives: 29.8 us -> none  [per_device(): top = lax.pmax(block_max, 'seq')]
    unnamed x8 -> x16, local copies, waits for them, and re-layouts: 0.6 us -> 13.5 us
    dot_general x6 -> x0, matrix products: 8.86 us -> none  [the longest x1 5.07 us: per_device(): jnp.dot(head_output.reshape(batch * drafts, heads_here * value_width), ou...]
  transfers between devices with their start and end apart: 1 -> 0, of which waited for: 1 -> 0; matrix products, arithmetic and copies ran while one was open for 0% -> 0% of each run, Pallas kernels for 0% -> 0%
where the time goes in v1:
time: 52 us; the launch traced here: 51.6 us
  Pallas kernels  37.3 us (72%)
  local copies, waits for them, and re-layouts  13.5 us (26%)
  between operations  0.83 us (2%)
    pallas_call x1, Pallas kernels, per_device(): pl.pallas_call(functools.partial(kernel, n, groups, heads, drafts), out_s...  37.3 us
    unnamed x16, local copies, waits for them, and re-layouts  13.5 us

profile of v1, /device:TPU:0, one launch (start us, length us, event | category | flops | bytes accessed | tf_op | source)
XLA Modules:
  0.0 51.6 jit_solution(4902224810311769949)
XLA Ops:
  0.0 0.0 copy-start.2
  0.0 0.0 copy-start.1
  0.0 0.0 copy-start.5
  0.0 0.0 copy-start
  0.0 0.0 copy-start.4
  0.0 0.0 copy-start.3
  0.8 0.8 %copy.11.ks_ref = f32[64,4]{1,0:T(8,128)S(1)} copy(f32[64,4]{0,1:T(4,128)} %param.16) | data formatting | bytes 2048 | tf_op args[6]
  1.6 0.8 %copy.12.vs_ref = f32[64,4]{1,0:T(8,128)S(1)} copy(f32[64,4]{0,1:T(4,128)} %param.18) | data formatting | bytes 2048 | tf_op args[8]
  2.3 11.3 %copy.13.w_hbm = bf16[8192,448]{1,0:T(8,128)(2,1)} copy(bf16[8192,448]{0,1:T(8,128)(2,1)} %param.19) | data formatting | bytes 14680064 | tf_op args[9]
  13.6 0.0 copy-done.2
  13.7 0.0 copy-done.1
  13.7 0.0 copy-done.5
  13.7 0.0 copy-done
  13.7 0.0 copy-done.4
  13.7 0.0 copy-done.3
  13.7 37.3 %shard_map.100 = bf16[4,448]{1,0:T(4,128)(2,1)S(1)} custom-call(bf16[256,128]{1,0:T(8,128)(2,1)S(1)} %bitcast.10, bf16[256,64]{1,0:T(8,128)(2,1)S(1)} %bitcast.11, bf16[512,512]{1,0:T(8,128)(2,1)S(1)} %bitcast.7, bf16[64,512]{1,0:T(8,128)(2,1)S(1)} %bitcast.12, s32[1]{0:T(128)S(6)} %copy.15.len_ref, bf16[2048,128]{1,0:T(8,128)(2,1)S(1)} %bitcast.8, ...), custom_call_target="tpu_custom_call" | custom-call | tf_op jit(solution)/shard_map/pallas_call | solution.py:279
  51.0 0.6 %copy.16 = bf16[1,4,448]{2,1,0:T(4,128)(2,1)} copy(bf16[1,4,448]{2,1,0:T(4,128)(2,1)S(1)} %bitcast.13) | data formatting | bytes 7168
Async XLA Ops:
  0.0 13.6 %copy-start.2 = (bf16[64,32,128]{2,1,0:T(8,128)(2,1)S(1)}, bf16[64,32,128]{2,1,0:T(8,128)(2,1)}, u32[]{:S(2)}) copy-start(bf16[64,32,128]{2,1,0:T(8,128)(2,1)} %param.17) | copy-start | bytes 1572868
  0.0 13.7 %copy-start.1 = (bf16[64,32,128]{2,1,0:T(8,128)(2,1)S(1)}, bf16[64,32,128]{2,1,0:T(8,128)(2,1)}, u32[]{:S(2)}) copy-start(bf16[64,32,128]{2,1,0:T(8,128)(2,1)} %param.15) | copy-start | bytes 1572868
  0.0 13.7 %copy-start.5 = (bf16[1,64,512]{2,1,0:T(8,128)(2,1)S(1)}, bf16[1,64,512]{2,1,0:T(8,128)(2,1)}, u32[]{:S(2)}) copy-start(bf16[1,64,512]{2,1,0:T(8,128)(2,1)} %param.13) | copy-start | bytes 196612
  0.0 13.7 %copy-start = (bf16[1,512,512]{2,1,0:T(8,128)(2,1)S(1)}, bf16[1,512,512]{2,1,0:T(8,128)(2,1)}, u32[]{:S(2)}) copy-start(bf16[1,512,512]{2,1,0:T(8,128)(2,1)} %param.12) | copy-start | bytes 1572868
  0.0 13.7 %copy-start.4 = (bf16[1,4,64,64]{3,2,1,0:T(8,128)(2,1)S(1)}, bf16[1,4,64,64]{3,2,1,0:T(8,128)(2,1)}, u32[]{:S(2)}) copy-start(bf16[1,4,64,64]{3,2,1,0:T(8,128)(2,1)} %param.11) | copy-start | bytes 98308
  0.0 13.7 %copy-start.3 = (bf16[1,4,64,128]{3,2,1,0:T(8,128)(2,1)S(1)}, bf16[1,4,64,128]{3,2,1,0:T(8,128)(2,1)}, u32[]{:S(2)}) copy-start(bf16[1,4,64,128]{3,2,1,0:T(8,128)(2,1)} %param.10) | copy-start | bytes 196612

commit v2 on v1

--- a/solution.py
+++ b/solution.py
@@ -16,11 +16,14 @@
 
 def scale_row(scale_ref, block, rows, heads):
     scales = scale_ref[...]
-    column = jnp.sum(
-        jnp.where(lax.broadcasted_iota(jnp.int32, scales.shape, 1) == block, scales, 0.0),
-        axis=1,
+    line = jnp.sum(
+        jnp.where(lax.broadcasted_iota(jnp.int32, scales.shape, 0) == block, scales, 0.0),
+        axis=0,
         keepdims=True,
     )
+    square = (heads, heads)
+    diagonal = lax.broadcasted_iota(jnp.int32, square, 0) == lax.broadcasted_iota(jnp.int32, square, 1)
+    column = jnp.sum(jnp.where(diagonal, line, 0.0), axis=1, keepdims=True)
     lane_head = lax.broadcasted_iota(jnp.int32, (heads, rows), 1) % heads
     own_head = lax.broadcasted_iota(jnp.int32, (heads, rows), 0)
     return jnp.sum(jnp.where(lane_head == own_head, column, 0.0), axis=0, keepdims=True)
@@ -225,7 +228,9 @@
     for k in range(heads):
         flat[:, k * width : (k + 1) * width] = heads_out[:, k, :].astype(BF16)
     w_load.wait()
-    final[group] = jnp.dot(flat[...], w[...], preferred_element_type=F32)
+    final[group] = lax.dot_general(
+        flat[...], w[...], (((1,), (1,)), ((), ())), preferred_element_type=F32
+    )
 
     def pair(j, at):
         peer = lax.rem(group + j, groups)
@@ -288,7 +293,7 @@
                 pltpu.VMEM((rope, positions), BF16),
                 pltpu.VMEM((heads * cols, nope), BF16),
                 pltpu.VMEM((heads * cols, width), BF16),
-                pltpu.VMEM(out_weight.shape, BF16),
+                pltpu.VMEM(out_weight.shape[::-1], BF16),
                 pltpu.VMEM((latent, positions), BF16),
                 pltpu.VMEM((width, heads * cols), BF16),
                 pltpu.VMEM((positions, rows), F32),
@@ -307,7 +312,7 @@
             + [dma((n,))] * 10
             + [dma((groups,))] * 2,
             compiler_params=pltpu.CompilerParams(
-                collective_id=0, has_side_effects=True, vmem_limit_bytes=48 * 1024 * 1024
+                collective_id=0, has_side_effects=True, vmem_limit_bytes=63 * 1024 * 1024
             ),
         )(
             query_nope.reshape(rows, nope),
@@ -316,10 +321,10 @@
             rope_keys.reshape(rope, positions),
             lengths,
             key_quant.reshape(heads * cols, nope),
-            key_scale,
+            key_scale.T,
             value_quant.reshape(heads * cols, width),
-            value_scale,
-            out_weight,
+            value_scale.T,
+            out_weight.T,
         )
         return result.reshape(batch, drafts, model)
 

time: 52 us -> 41.3 us (0.79)
  local copies, waits for them, and re-layouts: 13.5 us -> 1.28 us
  Pallas kernels: 37.3 us -> 39.1 us
    unnamed x16 -> x1, local copies, waits for them, and re-layouts: 13.5 us -> 1.28 us
    pallas_call x1, Pallas kernels: 37.3 us -> 39.1 us  [per_device(): pl.pallas_call(functools.partial(kernel, n, groups, heads, drafts), out_s...]
where the time goes in v2:
time: 41.3 us; the launch traced here: 41 us
  Pallas kernels  39.1 us (95%)
  local copies, waits for them, and re-layouts  1.28 us (3%)
  between operations  0.66 us (2%)
    pallas_call x1, Pallas kernels, per_device(): pl.pallas_call(functools.partial(kernel, n, groups, heads, drafts), out_s...  39.1 us
    unnamed x1, local copies, waits for them, and re-layouts  1.28 us

profile of v2, /device:TPU:0, one launch (start us, length us, event | category | flops | bytes accessed | tf_op | source)
XLA Modules:
  0.0 41.0 jit_solution(6960332693630956860)
XLA Ops:
  0.7 39.1 %shard_map.100 = bf16[4,448]{1,0:T(4,128)(2,1)} custom-call(bf16[256,128]{1,0:T(8,128)(2,1)} %bitcast.14, bf16[256,64]{1,0:T(8,128)(2,1)} %bitcast.15, bf16[512,512]{1,0:T(8,128)(2,1)} %bitcast.11, bf16[64,512]{1,0:T(8,128)(2,1)} %bitcast.16, s32[1]{0:T(128)S(6)} %copy.12.len_ref, bf16[2048,128]{1,0:T(8,128)(2,1)} %bitcast.12, f32[4,64]{1,0:T(4,128)} %bitcast.18, ...), custom_call_target="tpu_custom_call" | custom-call | tf_op jit(solution)/shard_map/pallas_call | solution.py:284
  39.8 1.3 %copy.13 = bf16[1,4,448]{2,1,0:T(4,128)(2,1)} copy(bf16[1,4,448]{2,1,0:T(4,128)(2,1)} %bitcast.17) | data formatting | bytes 7168

commit v3 on v2

--- a/solution.py
+++ b/solution.py
@@ -68,6 +68,7 @@
     in_sem,
     lat_send,
     lat_recv,
+    pass_send,
     st_send,
     st_recv,
     o_send,
@@ -92,7 +93,8 @@
         ((kq_hbm, kq), (q_hbm, q), (qr_hbm, qr), (rope_hbm, rope), (cache_hbm, cache), (vq_hbm, vq), (w_hbm, w))
     ):
         copy = pltpu.make_async_copy(src, dst, in_sem.at[i])
-        copy.start()
+        if dst is not w:
+            copy.start()
         loads.append(copy)
     kq_load, q_load, qr_load, rope_load, cache_load, vq_load, w_load = loads
 
@@ -171,14 +173,51 @@
     lat_all[me] = piece.astype(BF16)
 
     pl.semaphore_wait(barrier, n - 1 + groups - 1)
-    lat = (lambda peer: lat_all.at[me], lat_all, lat_send, lat_recv)
-    spread(*lat)
+
+    partner = me + 1 - 2 * lax.rem(me, 2)
+
+    def lat_copy(slot, peer, send):
+        return pltpu.make_async_remote_copy(
+            src_ref=lat_all.at[slot],
+            dst_ref=lat_all.at[slot],
+            send_sem=send,
+            recv_sem=lat_recv.at[slot],
+            device_id=(group, peer),
+            device_id_type=MESH,
+        )
+
+    def like(j):
+        return lax.rem(me + 2 * j, n)
+
+    def lat_go(j, c):
+        lat_copy(me, like(j), lat_send.at[like(j)]).start()
+        return c
+
+    def lat_pass(j, c):
+        lat_copy(like(j), partner, pass_send.at[like(j)]).wait_recv()
+        lat_copy(like(j), partner, pass_send.at[like(j)]).start()
+        return c
+
+    def lat_rest(j, c):
+        other = lax.rem(partner + 2 * j, n)
+        lat_copy(other, partner, pass_send.at[other]).wait_recv()
+        return c
+
+    def lat_drain(j, c):
+        lat_copy(me, like(j), lat_send.at[like(j)]).wait_send()
+        lat_copy(like(j), partner, pass_send.at[like(j)]).wait_send()
+        return c
+
+    lax.fori_loop(1, n // 2, lat_go, 0)
+    lat_copy(me, partner, lat_send.at[partner]).start()
+    w_load.start()
 
     qr_load.wait()
     rope_load.wait()
     base[...] = lax.dot_general(
         rope[...].T, qr[...], (((1,), (1,)), ((), ())), preferred_element_type=F32
     )
+    lax.fori_loop(1, n // 2, lat_pass, 0)
     cache_load.wait()
     cache_t[...] = cache[...].T
     vq_load.wait()
@@ -187,7 +226,7 @@
     horizon = len_ref[0] + lax.broadcasted_iota(jnp.int32, (positions, rows), 1) // heads
     visible = position < horizon
 
-    arrive(*lat)
+    lax.fori_loop(0, n // 2, lat_rest, 0)
     query_latent = lat_all[...].reshape(n * cols, rows)
     scores = (jnp.dot(cache[...], query_latent, preferred_element_type=F32) + base[...]) * factor
     block_max = jnp.max(jnp.where(visible, scores, neg_large), axis=0, keepdims=True)
@@ -248,8 +287,10 @@
     for j in range(1, groups):
         pair(j, False).wait_recv()
     out_ref[...] = jnp.sum(final[...], axis=0).astype(BF16)
-    for each in (lat, st, o, p, s):
+    for each in (st, o, p, s):
         drain(*each)
+    lax.fori_loop(1, n // 2, lat_drain, 0)
+    lat_copy(me, partner, lat_send.at[partner]).wait_send()
     for j in range(1, groups):
         pair(j, True).wait_send()
 
@@ -309,7 +350,7 @@
                 pltpu.VMEM((groups, drafts, model), F32),
                 dma((7,)),
             ]
-            + [dma((n,))] * 10
+            + [dma((n,))] * 11
             + [dma((groups,))] * 2,
             compiler_params=pltpu.CompilerParams(
                 collective_id=0, has_side_effects=True, vmem_limit_bytes=63 * 1024 * 1024

time: 41.3 us -> 40.2 us (0.973)
  Pallas kernels: 39.1 us -> 38 us
    pallas_call x1, Pallas kernels: 39.1 us -> 38 us  [per_device(): pl.pallas_call(functools.partial(kernel, n, groups, heads, drafts), out_s...]
where the time goes in v3:
time: 40.2 us; the launch traced here: 40 us
  Pallas kernels  38 us (95%)
  local copies, waits for them, and re-layouts  1.28 us (3%)
  between operations  0.66 us (2%)
    pallas_call x1, Pallas kernels, per_device(): pl.pallas_call(functools.partial(kernel, n, groups, heads, drafts), out_s...  38 us
    unnamed x1, local copies, waits for them, and re-layouts  1.28 us

profile of v3, /device:TPU:0, one launch (start us, length us, event | category | flops | bytes accessed | tf_op | source)
XLA Modules:
  0.0 40.0 jit_solution(18167443988940198919)
XLA Ops:
  0.7 38.0 %shard_map.100 = bf16[4,448]{1,0:T(4,128)(2,1)} custom-call(bf16[256,128]{1,0:T(8,128)(2,1)} %bitcast.14, bf16[256,64]{1,0:T(8,128)(2,1)} %bitcast.15, bf16[512,512]{1,0:T(8,128)(2,1)} %bitcast.11, bf16[64,512]{1,0:T(8,128)(2,1)} %bitcast.16, s32[1]{0:T(128)S(6)} %copy.12.len_ref, bf16[2048,128]{1,0:T(8,128)(2,1)} %bitcast.12, f32[4,64]{1,0:T(4,128)} %bitcast.18, ...), custom_call_target="tpu_custom_call" | custom-call | tf_op jit(solution)/shard_map/pallas_call | solution.py:325
  38.7 1.3 %copy.13 = bf16[1,4,448]{2,1,0:T(4,128)(2,1)} copy(bf16[1,4,448]{2,1,0:T(4,128)(2,1)} %bitcast.17) | data formatting | bytes 7168
